TPU v7x, 32 devices: a whole 2x2x4 slice. The times are simulated.
32 devices in a mesh: dp: 8 (over z, y), mp: 4 (over x, core).
Axes of the slice: x: 2, y: 2, z: 4, core: 2. Of those that a mesh axis runs over, the one named last changes fastest.
Arguments:
- inputs: bfloat16 [16384, 1024], P(('dp', 'mp')), may hold values from -6 to 6
- first_values: bfloat16 [16384, 8, 64], P('dp', 'mp'), may hold values from -6 to 6
- cotangent: bfloat16 [16384, 1024], P(('dp', 'mp')), may hold values from -6 to 6
- seq_lengths: int32 [32], P('dp'), may hold values from 0 to 1024, as said below
- value_owner: int32 [8], replicated, may hold values from 0 to 7, each once
- attn_norm_gain: float32 [1024], replicated, may hold values from 0.5 to 1.5
- attn_norm_bias: float32 [1024], replicated, may hold values from -3 to 3
- qkv_weight: bfloat16 [1024, 8, 5, 64], P(None, 'mp'), may hold values from -0.25 to 0.25
- qv_bias: float32 [8, 3, 64], P('mp'), may hold values from -3 to 3
- out_weight: bfloat16 [8, 2, 64, 1024], P('mp'), may hold values from -0.75 to 0.75
- out_bias: float32 [1024], replicated, may hold values from -3 to 3
- mlp_norm_gain: float32 [1024], replicated, may hold values from 0.5 to 1.5
- mlp_norm_bias: float32 [1024], replicated, may hold values from -3 to 3
- up_weight: bfloat16 [1024, 4096], P(None, 'mp'), may hold values from -0.1875 to 0.1875
- up_bias: float32 [4096], P('mp'), may hold values from -3 to 3
- down_weight: bfloat16 [4096, 1024], P('mp'), may hold values from -0.09375 to 0.09375
- down_bias: float32 [1024], replicated, may hold values from -3 to 3
Outputs:
- output: bfloat16 [16384, 1024], P(('dp', 'mp'))
- grad_inputs: bfloat16 [16384, 1024], P(('dp', 'mp'))
- grad_first_values: bfloat16 [16384, 8, 64], P('dp', 'mp')
- grad_attn_norm_gain: float32 [1024], replicated
- grad_attn_norm_bias: float32 [1024], replicated
- grad_qkv_weight: float32 [1024, 8, 5, 64], P(None, 'mp')
- grad_qv_bias: float32 [8, 3, 64], P('mp')
- grad_out_weight: float32 [8, 2, 64, 1024], P('mp')
- grad_out_bias: float32 [1024], replicated
- grad_mlp_norm_gain: float32 [1024], replicated
- grad_mlp_norm_bias: float32 [1024], replicated
- grad_up_weight: float32 [1024, 4096], P(None, 'mp')
- grad_up_bias: float32 [4096], P('mp')
- grad_down_weight: float32 [4096, 1024], P('mp')
- grad_down_bias: float32 [1024], replicated
Inputs may be any that keep to these rules, and one draw needn't show every extreme that they name: `seq_lengths`: each data group's 4 entries, in row order, are the lengths of the sequences packed into its 2048 rows: each 512 or 1024, then zeros for unused slots; they sum to 2048, and some group holds a sequence of 1024. A permutation: skip-value head p reuses the first layer's value head value_owner[p].
All inputs are finite; a program needn't handle non-finite values.
Results may differ from a plain program's by a relative error of at most 0.019.
Values may be sent and summed in bfloat16 or wider, within the bound.
A program may use at most 128 MiB of HBM per device.

v0:
```python
import jax
import jax.numpy as jnp
from jax import lax
from jax.sharding import PartitionSpec as P

SHORT = 512
EPSILON = 1e-05
MASKED = -1e30
GELU_C = 0.7978845608028654


def layer_norm(values, scale_gain, scale_bias):
    average = jnp.mean(values, axis=-1, keepdims=True)
    centered = values - average
    variance = jnp.mean(centered * centered, axis=-1, keepdims=True)
    return centered * lax.rsqrt(variance + EPSILON) * scale_gain + scale_bias


def gelu_tanh(values):
    return 0.5 * values * (1.0 + jnp.tanh(GELU_C * (values + 0.044715 * values * values * values)))


def row_starts(lengths, group_rows):
    ends = jnp.cumsum(lengths)
    begins = ends - lengths
    positions = jnp.arange(group_rows, dtype=jnp.int32)
    inside = begins[None, :] <= positions[:, None]
    return jnp.max(jnp.where(inside, begins[None, :], 0), axis=1)


def block_mask(starts, first_row, block_rows, span):
    own_rows = first_row + jnp.arange(block_rows, dtype=jnp.int32)
    key_rows = first_row - (span - block_rows) + jnp.arange(span, dtype=jnp.int32)
    begin = lax.dynamic_slice_in_dim(starts, first_row, block_rows, 0)
    return (key_rows[None, :] >= begin[:, None]) & (key_rows[None, :] <= own_rows[:, None])


def rows_product(left, right):
    return lax.dot_general(
        left, right, (((0,), (0,)), ((), ())), preferred_element_type=jnp.float32
    )


def back_product(left, weight):
    return lax.dot_general(
        left, weight, (((1,), (1,)), ((), ())), preferred_element_type=jnp.float32
    )


def padded_pair(keys, values_in, long_len):
    zero_pad = jnp.zeros((long_len,) + keys.shape[1:], keys.dtype)
    return (jnp.concatenate([zero_pad, keys], 0), jnp.concatenate([zero_pad, values_in], 0))


def attend_forward(queries, keys, values_in, starts, long_len, block_rows):
    group_rows, heads, width = queries.shape
    span = long_len + block_rows
    scale = width ** (-0.5)
    keys_pad, values_pad = padded_pair(keys, values_in, long_len)

    def one_block(block_index):
        first_row = block_index * block_rows
        query_blk = lax.dynamic_slice_in_dim(queries, first_row, block_rows, 0)
        key_blk = lax.dynamic_slice_in_dim(keys_pad, first_row, span, 0)
        value_blk = lax.dynamic_slice_in_dim(values_pad, first_row, span, 0)
        allowed = block_mask(starts, first_row, block_rows, span)
        scores = (
            jnp.einsum("qhd,khd->hqk", query_blk, key_blk, preferred_element_type=jnp.float32)
            * scale
        )
        scores = jnp.where(allowed[None], scores, MASKED)
        top_score = jnp.max(scores, axis=-1, keepdims=True)
        weights = jnp.exp(scores - top_score)
        totals = jnp.sum(weights, axis=-1, keepdims=True)
        probs = (weights / totals).astype(jnp.bfloat16)
        mixed = jnp.einsum("hqk,khd->qhd", probs, value_blk, preferred_element_type=jnp.float32)
        return (mixed.astype(jnp.bfloat16), top_score[..., 0] + jnp.log(totals[..., 0]))

    mixed, log_totals = lax.map(one_block, jnp.arange(group_rows // block_rows, dtype=jnp.int32))
    return (mixed.reshape(group_rows, heads, width), log_totals)


def attend_backward(queries, keys, values_in, grad_mixed, log_totals, starts, long_len, block_rows):
    group_rows, heads, width = queries.shape
    span = long_len + block_rows
    scale = width ** (-0.5)
    keys_pad, values_pad = padded_pair(keys, values_in, long_len)

    def one_block(carried, block_index):
        grad_keys, grad_values = carried
        first_row = block_index * block_rows
        query_blk = lax.dynamic_slice_in_dim(queries, first_row, block_rows, 0)
        key_blk = lax.dynamic_slice_in_dim(keys_pad, first_row, span, 0)
        value_blk = lax.dynamic_slice_in_dim(values_pad, first_row, span, 0)
        grad_blk = lax.dynamic_slice_in_dim(grad_mixed, first_row, block_rows, 0)
        allowed = block_mask(starts, first_row, block_rows, span)
        scores = (
            jnp.einsum("qhd,khd->hqk", query_blk, key_blk, preferred_element_type=jnp.float32)
            * scale
        )
        probs = jnp.where(allowed[None], jnp.exp(scores - log_totals[block_index][:, :, None]), 0.0)
        grad_probs = jnp.einsum(
            "qhd,khd->hqk", grad_blk, value_blk, preferred_element_type=jnp.float32
        )
        inner = jnp.sum(probs * grad_probs, axis=-1, keepdims=True)
        grad_scores = (probs * (grad_probs - inner)).astype(jnp.bfloat16)
        grad_query = (
            jnp.einsum("hqk,khd->qhd", grad_scores, key_blk, preferred_element_type=jnp.float32)
            * scale
        )
        grad_key = (
            jnp.einsum("hqk,qhd->khd", grad_scores, query_blk, preferred_element_type=jnp.float32)
            * scale
        )
        grad_value = jnp.einsum(
            "hqk,qhd->khd", probs.astype(jnp.bfloat16), grad_blk, preferred_element_type=jnp.float32
        )
        grad_keys = lax.dynamic_update_slice_in_dim(
            grad_keys,
            lax.dynamic_slice_in_dim(grad_keys, first_row, span, 0) + grad_key,
            first_row,
            0,
        )
        grad_values = lax.dynamic_update_slice_in_dim(
            grad_values,
            lax.dynamic_slice_in_dim(grad_values, first_row, span, 0) + grad_value,
            first_row,
            0,
        )
        return ((grad_keys, grad_values), grad_query)

    zero_grads = jnp.zeros((long_len + group_rows, heads, width), jnp.float32)
    (grad_keys, grad_values), grad_queries = lax.scan(
        one_block, (zero_grads, zero_grads), jnp.arange(group_rows // block_rows, dtype=jnp.int32)
    )
    return (
        grad_queries.reshape(group_rows, heads, width),
        grad_keys[long_len:],
        grad_values[long_len:],
    )


def body(
    inputs,
    first_values,
    cotangent,
    seq_lengths,
    value_owner,
    attn_norm_gain,
    attn_norm_bias,
    qkv_weight,
    qv_bias,
    out_weight,
    out_bias,
    mlp_norm_gain,
    mlp_norm_bias,
    up_weight,
    up_bias,
    down_weight,
    down_bias,
):
    local_rows = inputs.shape[0]
    model_width = inputs.shape[1]
    group_rows = local_rows * lax.axis_size("mp")
    pairs_dev = qkv_weight.shape[1]
    head_size = qkv_weight.shape[3]
    heads_dev = 2 * pairs_dev
    all_pairs = value_owner.shape[0]
    long_len = 2 * SHORT
    block_rows = min(512, group_rows)
    starts = row_starts(seq_lengths, group_rows)
    all_first = lax.all_gather(first_values, "mp", axis=1, tiled=True)
    owners = lax.dynamic_slice_in_dim(value_owner, lax.axis_index("mp") * pairs_dev, pairs_dev, 0)
    skip_values = jnp.take(all_first, owners, axis=1)
    qkv_flat = qkv_weight.reshape(model_width, pairs_dev * 5 * head_size)
    out_flat = out_weight.reshape(heads_dev * head_size, model_width)

    def run_forward(layer_in):
        inputs_f = layer_in.astype(jnp.float32)
        normed_one = layer_norm(inputs_f, attn_norm_gain, attn_norm_bias).astype(jnp.bfloat16)
        rows_one = lax.all_gather(normed_one, "mp", axis=0, tiled=True)
        projected = jnp.dot(rows_one, qkv_flat, preferred_element_type=jnp.float32)
        projected = projected.reshape(group_rows, pairs_dev, 5, head_size)
        queries = (projected[:, :, 0:2] + qv_bias[None, :, 0:2]).astype(jnp.bfloat16)
        queries = queries.reshape(group_rows, heads_dev, head_size)
        keys = projected[:, :, 2:4].astype(jnp.bfloat16).reshape(group_rows, heads_dev, head_size)
        fresh = (projected[:, :, 4] + qv_bias[None, :, 2]).astype(jnp.bfloat16)
        values_all = jnp.stack([fresh, skip_values], axis=2).reshape(
            group_rows, heads_dev, head_size
        )
        mixed, log_totals = attend_forward(queries, keys, values_all, starts, long_len, block_rows)
        mixed_flat = mixed.reshape(group_rows, heads_dev * head_size)
        picked = mixed_flat
        residual = (
            inputs_f
            + lax.psum_scatter(
                jnp.dot(picked, out_flat, preferred_element_type=jnp.float32).astype(jnp.bfloat16),
                "mp",
                scatter_dimension=0,
                tiled=True,
            ).astype(jnp.float32)
            + out_bias
        )
        normed_two = layer_norm(residual, mlp_norm_gain, mlp_norm_bias).astype(jnp.bfloat16)
        rows_two = lax.all_gather(normed_two, "mp", axis=0, tiled=True)
        hidden_pre = jnp.dot(rows_two, up_weight, preferred_element_type=jnp.float32) + up_bias
        hidden = gelu_tanh(hidden_pre).astype(jnp.bfloat16)
        picked = hidden
        layer_out = (
            residual
            + lax.psum_scatter(
                jnp.dot(picked, down_weight, preferred_element_type=jnp.float32).astype(
                    jnp.bfloat16
                ),
                "mp",
                scatter_dimension=0,
                tiled=True,
            ).astype(jnp.float32)
            + down_bias
        )
        return (
            layer_out,
            inputs_f,
            residual,
            rows_one,
            queries,
            keys,
            values_all,
            log_totals,
            mixed_flat,
            rows_two,
            hidden_pre,
            hidden,
        )

    saved = run_forward(inputs)
    output = saved[0].astype(jnp.bfloat16)
    again_in = lax.optimization_barrier((inputs, saved[0]))[0]
    saved = run_forward(again_in)
    (
        inputs_f,
        residual,
        rows_one,
        queries,
        keys,
        values_all,
        log_totals,
        mixed_flat,
        rows_two,
        hidden_pre,
        hidden,
    ) = saved[1:]
    grad_out_f = cotangent.astype(jnp.float32)
    grad_rows = lax.all_gather(cotangent, "mp", axis=0, tiled=True)
    grad_hidden = back_product(grad_rows, down_weight)
    gelu_pair = jax.vjp(gelu_tanh, hidden_pre)
    grad_pre = gelu_pair[1](grad_hidden)[0].astype(jnp.bfloat16)
    grad_down_weight = rows_product(hidden, grad_rows)
    grad_up_weight = rows_product(rows_two, grad_pre)
    grad_up_bias = jnp.sum(grad_pre.astype(jnp.float32), axis=0)
    grad_down_bias = jnp.sum(grad_out_f, axis=0)
    grad_normed_two = lax.psum_scatter(
        back_product(grad_pre, up_weight).astype(jnp.bfloat16),
        "mp",
        scatter_dimension=0,
        tiled=True,
    ).astype(jnp.float32)
    norm_two_pair = jax.vjp(layer_norm, residual, mlp_norm_gain, mlp_norm_bias)
    grad_through, grad_mlp_norm_gain, grad_mlp_norm_bias = norm_two_pair[1](grad_normed_two)
    grad_residual = grad_out_f + grad_through
    grad_out_bias = jnp.sum(grad_residual, axis=0)
    resid_rows = lax.all_gather(grad_residual.astype(jnp.bfloat16), "mp", axis=0, tiled=True)
    grad_out_weight = rows_product(mixed_flat, resid_rows).reshape(out_weight.shape)
    grad_mixed = back_product(resid_rows, out_flat).astype(jnp.bfloat16)
    grad_mixed = grad_mixed.reshape(group_rows, heads_dev, head_size)
    grad_query, grad_key, grad_value = attend_backward(
        queries, keys, values_all, grad_mixed, log_totals, starts, long_len, block_rows
    )
    grad_value = grad_value.reshape(group_rows, pairs_dev, 2, head_size)
    grad_projected = jnp.concatenate(
        [
            grad_query.reshape(group_rows, pairs_dev, 2, head_size),
            grad_key.reshape(group_rows, pairs_dev, 2, head_size),
            grad_value[:, :, 0:1],
        ],
        axis=2,
    ).astype(jnp.bfloat16)
    grad_qv_bias = jnp.concatenate(
        [
            jnp.sum(grad_projected[:, :, 0:2].astype(jnp.float32), axis=0),
            jnp.sum(grad_projected[:, :, 4:5].astype(jnp.float32), axis=0),
        ],
        axis=1,
    )
    grad_flat = grad_projected.reshape(group_rows, pairs_dev * 5 * head_size)
    grad_qkv_weight = rows_product(rows_one, grad_flat).reshape(qkv_weight.shape)
    grad_normed_one = lax.psum_scatter(
        back_product(grad_flat, qkv_flat).astype(jnp.bfloat16),
        "mp",
        scatter_dimension=0,
        tiled=True,
    ).astype(jnp.float32)
    norm_one_pair = jax.vjp(layer_norm, inputs_f, attn_norm_gain, attn_norm_bias)
    grad_through_one, grad_attn_norm_gain, grad_attn_norm_bias = norm_one_pair[1](grad_normed_one)
    grad_inputs = (grad_residual + grad_through_one).astype(jnp.bfloat16)
    every_skip = lax.all_gather(grad_value[:, :, 1].astype(jnp.bfloat16), "mp", axis=1, tiled=True)
    owned = lax.axis_index("mp") * pairs_dev + jnp.arange(pairs_dev, dtype=jnp.int32)
    every_pair = jnp.arange(all_pairs, dtype=jnp.int32)
    inverse = jnp.sum(
        jnp.where(value_owner[None, :] == owned[:, None], every_pair[None, :], 0), axis=1
    )
    grad_first = jnp.take(every_skip, inverse, axis=1)
    weight_sums = (
        lax.psum(grad_qkv_weight.astype(jnp.bfloat16), "dp").astype(jnp.float32),
        lax.psum(grad_qv_bias.astype(jnp.bfloat16), "dp").astype(jnp.float32),
        lax.psum(grad_out_weight.astype(jnp.bfloat16), "dp").astype(jnp.float32),
        lax.psum(grad_up_weight.astype(jnp.bfloat16), "dp").astype(jnp.float32),
        lax.psum(grad_up_bias.astype(jnp.bfloat16), "dp").astype(jnp.float32),
        lax.psum(grad_down_weight.astype(jnp.bfloat16), "dp").astype(jnp.float32),
    )
    norm_sums = lax.psum(
        (
            grad_attn_norm_gain,
            grad_attn_norm_bias,
            grad_out_bias,
            grad_mlp_norm_gain,
            grad_mlp_norm_bias,
            grad_down_bias,
        ),
        ("dp", "mp"),
    )
    return (
        output,
        grad_inputs,
        grad_first,
        norm_sums[0],
        norm_sums[1],
        weight_sums[0],
        weight_sums[1],
        weight_sums[2],
        norm_sums[2],
        norm_sums[3],
        norm_sums[4],
        weight_sums[3],
        weight_sums[4],
        weight_sums[5],
        norm_sums[5],
    )


def solution(mesh):
    return jax.shard_map(
        body,
        mesh=mesh,
        in_specs=(
            P(("dp", "mp"), None),
            P("dp", "mp", None),
            P(("dp", "mp"), None),
            P("dp"),
            P(),
            P(),
            P(),
            P(None, "mp", None, None),
            P("mp", None, None),
            P("mp", None, None, None),
            P(),
            P(),
            P(),
            P(None, "mp"),
            P("mp"),
            P("mp", None),
            P(),
        ),
        out_specs=(
            P(("dp", "mp"), None),
            P(("dp", "mp"), None),
            P("dp", "mp", None),
            P(),
            P(),
            P(None, "mp", None, None),
            P("mp", None, None),
            P("mp", None, None, None),
            P(),
            P(),
            P(),
            P(None, "mp"),
            P("mp"),
            P("mp", None),
            P(),
        ),
        check_vma=False,
    )
```

profile of v0, /device:TPU:0, one launch (start us, length us, event | category | flops | bytes accessed | tf_op | source)
XLA Modules:
  0.0 1232.0 jit_solution(12711491678477917356)
XLA Ops:
  13.3 21.6 %all-gather.12.cloned.1.call-done = bf16[2048,8,64]{0,2,1:T(8,128)(2,1)} async-done(((bf16[2048,2,64]{0,2,1:T(8,128)(2,1)}), bf16[2048,8,64]{0,2,1:T(8,128)(2,1)}) %all-gather.12.cloned.1.call-update) | async-done | bytes 2097168 | tf_op jit(solution)/shard_map/all_gather | solution.py:172
  38.0 33.5 %all-gather.10.cloned.1.call-done = bf16[2048,1024]{1,0:T(8,128)(2,1)} async-done(((bf16[512,1024]{1,0:T(8,128)(2,1)}), bf16[2048,1024]{1,0:T(8,128)(2,1)}) %all-gather.10.cloned.1.call-update) | async-done | bytes 4194320 | tf_op jit(solution)/shard_map/all_gather | solution.py:181
  81.7 132.5 %while.42 = (s32[]{:T(128)}, bf16[4,512,4,64]{1,3,2,0:T(8,128)(2,1)}, s32[4]{0:T(128)S(1)}, bf16[3072,4,64]{0,2,1:T(8,128)(2,1)}, s32[2048]{0:T(1024)S(1)}, /*in...) while((s32[]{:T(128)}, ...), condition=%wide.region_7.9_spmd, body=%wide.region_4.8_spmd.sunk | while | flops 832966144 | bytes 60332316 | solution.py:79
  91.2 16.2 %fusion.196 = (f32[4,512]{1,0:T(4,128)S(1)}, f32[4,512,1536]{2,1,0:T(8,128)}) fusion(f32[4,512,1536]{2,1,0:T(8,128)} %fusion.195, pred[512,1536]{1,0:T(8,128)(4,1)S(1)} %compare_and_fusion.8), kind=kOutput, calls=%fused_computation.224.clone.1 | output fusion | flops 18875904 | bytes 25960448 | tf_op jit(solution)/shard_map/while/body/eval_jaxpr/sub | solution.py:73
  124.4 16.2 %fusion.196 = (f32[4,512]{1,0:T(4,128)S(1)}, f32[4,512,1536]{2,1,0:T(8,128)}) fusion(f32[4,512,1536]{2,1,0:T(8,128)} %fusion.195, pred[512,1536]{1,0:T(8,128)(4,1)S(1)} %compare_and_fusion.8), kind=kOutput, calls=%fused_computation.224.clone.1 | output fusion | flops 18875904 | bytes 25960448 | tf_op jit(solution)/shard_map/while/body/eval_jaxpr/sub | solution.py:73
  157.5 16.2 %fusion.196 = (f32[4,512]{1,0:T(4,128)S(1)}, f32[4,512,1536]{2,1,0:T(8,128)}) fusion(f32[4,512,1536]{2,1,0:T(8,128)} %fusion.195, pred[512,1536]{1,0:T(8,128)(4,1)S(1)} %compare_and_fusion.8), kind=kOutput, calls=%fused_computation.224.clone.1 | output fusion | flops 18875904 | bytes 25960448 | tf_op jit(solution)/shard_map/while/body/eval_jaxpr/sub | solution.py:73
  190.6 16.2 %fusion.196 = (f32[4,512]{1,0:T(4,128)S(1)}, f32[4,512,1536]{2,1,0:T(8,128)}) fusion(f32[4,512,1536]{2,1,0:T(8,128)} %fusion.195, pred[512,1536]{1,0:T(8,128)(4,1)S(1)} %compare_and_fusion.8), kind=kOutput, calls=%fused_computation.224.clone.1 | output fusion | flops 18875904 | bytes 25960448 | tf_op jit(solution)/shard_map/while/body/eval_jaxpr/sub | solution.py:73
  220.2 44.5 %reduce-scatter.6.cloned.1.call-done = bf16[512,1024]{1,0:T(8,128)(2,1)} async-done(((bf16[2048,1024]{1,0:T(8,128)(2,1)}), bf16[512,1024]{1,0:T(8,128)(2,1)}) %reduce-scatter.6.cloned.1.call-update) | async-done | bytes 1048592 | tf_op jit(solution)/shard_map/reduce_scatter | solution.py:196
  268.6 34.6 %all-gather.14.cloned.1.call-done = bf16[2048,1024]{1,0:T(8,128)(2,1)} async-done(((bf16[512,1024]{1,0:T(8,128)(2,1)}), bf16[2048,1024]{1,0:T(8,128)(2,1)}) %all-gather.14.cloned.1.call-update) | async-done | bytes 4194320 | tf_op jit(solution)/shard_map/all_gather | solution.py:205
  303.2 12.9 %fusion.81 = bf16[2048,1024]{1,0:T(8,128)(2,1)} fusion(bf16[1024,1024]{1,0:T(8,128)(2,1)} %param.40, f32[1024]{0:T(1024)S(1)} %copy-done.60, bf16[2048,1024]{1,0:T(8,128)(2,1)} %all-gather.14.cloned.1.call-done, bf16[1024,1024]{1,0:T(8,128)(2,1)S(1)} %copy-done), kind=kOutput, calls=%fused_computation.106 | convolution fusion | flops 8613003264 | bytes 12587008 | tf_op jit(solution)/shard_map/dot_general | solution.py:212
  316.2 44.7 %reduce-scatter.8.cloned.1.call-done = bf16[512,1024]{1,0:T(8,128)(2,1)} async-done(((bf16[2048,1024]{1,0:T(8,128)(2,1)}), bf16[512,1024]{1,0:T(8,128)(2,1)}) %reduce-scatter.8.cloned.1.call-update) | async-done | bytes 1048592 | tf_op jit(solution)/shard_map/reduce_scatter | solution.py:211
  367.6 34.3 %all-gather.16.cloned.1.call-done = bf16[2048,1024]{1,0:T(8,128)(2,1)} async-done(((bf16[512,1024]{1,0:T(8,128)(2,1)}), bf16[2048,1024]{1,0:T(8,128)(2,1)}) %all-gather.16.cloned.1.call-update) | async-done | bytes 4194320 | tf_op jit(solution)/shard_map/all_gather | solution.py:181
  412.4 55.7 %while.43 = (s32[]{:T(128)}, bf16[4,512,4,64]{1,3,2,0:T(8,128)(2,1)}, f32[4,4,512]{2,1,0:T(4,128)S(1)}, s32[4]{0:T(128)S(1)}, bf16[3072,4,64]{0,2,1:T(8,128)(2,1...) while((s32[]{:T(128)}, ...), condition=%wide.region_17.19_spmd, body=%wide.region_14.18_spmd.sunk | while | flops 845545472 | bytes 49371432 | solution.py:79
  475.3 44.2 %reduce-scatter.10.cloned.1.call-done = bf16[512,1024]{1,0:T(8,128)(2,1)} async-done(((bf16[2048,1024]{1,0:T(8,128)(2,1)}), bf16[512,1024]{1,0:T(8,128)(2,1)}) %reduce-scatter.10.cloned.1.call-update) | async-done | bytes 1048592 | tf_op jit(solution)/shard_map/reduce_scatter | solution.py:196
  524.3 33.8 %all-gather.18.cloned.1.call-done = bf16[2048,1024]{1,0:T(8,128)(2,1)} async-done(((bf16[512,1024]{1,0:T(8,128)(2,1)}), bf16[2048,1024]{1,0:T(8,128)(2,1)}) %all-gather.18.cloned.1.call-update) | async-done | bytes 4194320 | tf_op jit(solution)/shard_map/all_gather | solution.py:205
  567.1 27.1 %all-gather.20.cloned.1.call-done = bf16[2048,1024]{1,0:T(8,128)(2,1)} async-done(((bf16[512,1024]{1,0:T(8,128)(2,1)}), bf16[2048,1024]{1,0:T(8,128)(2,1)}) %all-gather.20.cloned.1.call-update) | async-done | bytes 4194320 | tf_op jit(solution)/shard_map/all_gather | solution.py:254
  594.2 15.5 %fusion.141 = (bf16[1024]{0:T(1024)(128)(2,1)}, bf16[2048,1024]{1,0:T(8,128)(2,1)S(1)}) fusion(f32[2048,1024]{1,0:T(8,128)} %fusion.146, f32[1024]{0:T(1024)S(1)} %copy-done.61, bf16[2048,1024]{1,0:T(8,128)(2,1)} %all-gather.20.cloned.1.call-done, bf16[1024,1024]{1,0:T(8,128)(2,1)} %param.40), kind=kOutput, calls=%fused_computation.222 | convolution fusion | flops 4349492224 | bytes 18880512 | tf_op jit(solution)/shard_map/dot_general | solution.py:45
  618.1 44.5 %reduce-scatter.12.cloned.1.call-done = bf16[512,1024]{1,0:T(8,128)(2,1)} async-done(((bf16[2048,1024]{1,0:T(8,128)(2,1)}), bf16[512,1024]{1,0:T(8,128)(2,1)}) %reduce-scatter.12.cloned.1.call-update) | async-done | bytes 1048592 | tf_op jit(solution)/shard_map/reduce_scatter | solution.py:262
  681.5 25.1 %all-gather.22.cloned.1.call-done = bf16[2048,1024]{1,0:T(8,128)(2,1)} async-done(((bf16[512,1024]{1,0:T(8,128)(2,1)}), bf16[2048,1024]{1,0:T(8,128)(2,1)}) %all-gather.22.cloned.1.call-update) | async-done | bytes 4194320 | tf_op jit(solution)/shard_map/all_gather | solution.py:272
  715.1 180.7 %while.44 = (s32[]{:T(128)}, f32[3072,4,64]{0,2,1:T(8,128)}, f32[3072,4,64]{0,2,1:T(8,128)}, bf16[4,512,4,64]{1,0,3,2:T(4,128)(2,1)}, s32[4]{0:T(128)S(1)}, /*in...) while((s32[]{:T(128)}, f32[3072,4,64]{0,2,1:T(8,128)}, ...), condition=%wide.region_26.28_spmd, body=%wide.region_24.27_spmd.sunk | while | flops 2045378560 | bytes 163641856 | solution.py:133
  935.6 22.7 %all-reduce.5 = (bf16[2,3,64]{2,1,0:T(4,128)(2,1)S(1)}, bf16[1024]{0:T(1024)(128)(2,1)S(1)}) all-reduce(bf16[2,3,64]{2,1,0:T(4,128)(2,1)S(1)} %pad_maximum_fusion.2, bf16[1024]{0:T(1024)(128)(2,1)S(1)} %copy-done.54), channel_id=1, replica_groups=mesh['dp'=8,'mp'=4] {'dp'}, use_global_device_ids=true, to_apply=%region_38.40 | all-reduce | flops 1408 | bytes 5632 | tf_op jit(solution)/shard_map/psum | solution.py:315
  962.6 169.5 %all-reduce.9.cloned.1.call-done = (bf16[1024,2,5,64]{0,3,2,1:T(8,128)(2,1)}, bf16[2,2,64,1024]{3,2,1,0:T(8,128)(2,1)}, bf16[1024,1024]{1,0:T(8,128)(2,1)}, bf16[1024,1024]{1,0:T(8,128)(2,1)}) async-done(((bf16[1024,2,5,64]{0,3,2,1:T(8,128)(2,1)}, bf16[2,2,64,1024]{3,2,1,0:T(8,128)(2,1)}, bf16[1024,1024]{1,0:T(8,128)(2,1)}, bf16[1024,1024]{1,0:T(8,128)(2,1)}), (bf16[1024,2,5,64]{0,3,2,1:T(8,128)(2,1)}, ...) | async-done | bytes 6029328 | tf_op jit(solution)/shard_map/psum | solution.py:314
  1143.0 35.2 %reduce-scatter.14.cloned.1.call-done = bf16[512,1024]{1,0:T(8,128)(2,1)} async-done(((bf16[2048,1024]{1,0:T(8,128)(2,1)}), bf16[512,1024]{1,0:T(8,128)(2,1)}) %reduce-scatter.14.cloned.1.call-update) | async-done | bytes 1048592 | tf_op jit(solution)/shard_map/reduce_scatter | solution.py:297
  1181.4 39.9 %all-reduce.4 = (f32[1024]{0:T(1024)}, f32[1024]{0:T(1024)}, f32[1024]{0:T(1024)}, f32[1024]{0:T(1024)}, f32[1024]{0:T(1024)}, /*index=5*/f32[1024]{0:T(1024)}) all-reduce(f32[1024]{0:T(1024)S(1)} %get-tuple-element.386, f32[1024]{0:T(1024)S(1)} %get-tuple-element.390, ...), channel_id=1, replica_groups=mesh['dp'=8,'mp'=4] {'dp','mp'}, use_global_device_ids=true, to_apply=%region_32.34 | all-reduce | flops 6144 | bytes 49152 | tf_op jit(solution)/shard_map/psum | solution.py:321
  (423 shorter events, 451.9 us)
Async XLA Ops:
  7.2 296.0 %copy-start = (bf16[1024,1024]{1,0:T(8,128)(2,1)S(1)}, bf16[1024,1024]{1,0:T(8,128)(2,1)}, u32[]{:S(2)}) copy-start(bf16[1024,1024]{1,0:T(8,128)(2,1)} %param.38) | copy-start | bytes 6291460
  7.2 27.7 %all-gather.12.cloned.1.call-start = ((), (), s32[]{:S(2)}) async-start(), calls=%async_computation.6 | async-start | bytes 2621440 | tf_op jit(solution)/shard_map/all_gather | solution.py:172
  8.0 63.5 %all-gather.10.cloned.1.call-start = ((), (), s32[]{:S(2)}) async-start(), calls=%async_computation.5 | async-start | bytes 5242880 | tf_op jit(solution)/shard_map/all_gather | solution.py:181
  12.8 251.8 %reduce-scatter.6.cloned.1.call-start = ((), (), s32[]{:S(2)}) async-start(), calls=%async_computation.7 | async-start | bytes 5242880 | tf_op jit(solution)/shard_map/reduce_scatter | solution.py:196
  13.0 63.9 %copy-start.40 = (f32[2,2,64]{2,1,0:T(2,128)}, f32[2,2,64]{2,1,0:T(2,128)S(1)}, u32[]{:S(2)}) copy-start(f32[2,2,64]{2,1,0:T(2,128)S(1)} %copy.44) | copy-start | bytes 3076
  13.3 63.5 %copy-start.50 = (f32[2,64]{1,0:T(2,128)}, f32[2,64]{1,0:T(2,128)S(1)}, u32[]{:S(2)}) copy-start(f32[2,64]{1,0:T(2,128)S(1)} %slice_bitcast_fusion) | copy-start | bytes 1540
  219.9 47.1 %copy-start.29 = (f32[1024]{0:T(1024)S(1)}, f32[1024]{0:T(1024)}, u32[]{:S(2)}) copy-start(f32[1024]{0:T(1024)} %param.36) | copy-start | bytes 12292
  219.9 47.1 %copy-start.44 = (f32[1024]{0:T(1024)S(1)}, f32[1024]{0:T(1024)}, u32[]{:S(2)}) copy-start(f32[1024]{0:T(1024)} %param.37) | copy-start | bytes 12292
  219.9 83.3 %all-gather.14.cloned.1.call-start = ((), (), s32[]{:S(2)}) async-start(), calls=%async_computation.8 | async-start | bytes 5242880 | tf_op jit(solution)/shard_map/all_gather | solution.py:205
  268.6 92.3 %reduce-scatter.8.cloned.1.call-start = ((), (), s32[]{:S(2)}) async-start(), calls=%async_computation.9 | async-start | bytes 5242880 | tf_op jit(solution)/shard_map/reduce_scatter | solution.py:211
  316.2 49.7 %copy-start.32 = (f32[1024]{0:T(1024)S(1)}, f32[1024]{0:T(1024)}, u32[]{:S(2)}) copy-start(f32[1024]{0:T(1024)} %param.30) | copy-start | bytes 12292
  316.2 49.7 %copy-start.43 = (f32[1024]{0:T(1024)S(1)}, f32[1024]{0:T(1024)}, u32[]{:S(2)}) copy-start(f32[1024]{0:T(1024)} %param.31) | copy-start | bytes 12292
  316.2 85.8 %all-gather.16.cloned.1.call-start = ((), (), s32[]{:S(2)}) async-start(), calls=%async_computation.10 | async-start | bytes 5242880 | tf_op jit(solution)/shard_map/all_gather | solution.py:181
  367.3 152.2 %reduce-scatter.10.cloned.1.call-start = ((), (), s32[]{:S(2)}) async-start(), calls=%async_computation.11 | async-start | bytes 5242880 | tf_op jit(solution)/shard_map/reduce_scatter | solution.py:196
  474.8 47.1 %copy-start.30 = (f32[1024]{0:T(1024)S(1)}, f32[1024]{0:T(1024)}, u32[]{:S(2)}) copy-start(f32[1024]{0:T(1024)} %param.36) | copy-start | bytes 12292
  474.8 47.0 %copy-start.45 = (f32[1024]{0:T(1024)S(1)}, f32[1024]{0:T(1024)}, u32[]{:S(2)}) copy-start(f32[1024]{0:T(1024)} %param.37) | copy-start | bytes 12292
  474.8 83.3 %all-gather.18.cloned.1.call-start = ((), (), s32[]{:S(2)}) async-start(), calls=%async_computation.12 | async-start | bytes 5242880 | tf_op jit(solution)/shard_map/all_gather | solution.py:205
  523.5 70.7 %all-gather.20.cloned.1.call-start = ((), (), s32[]{:S(2)}) async-start(), calls=%async_computation.13 | async-start | bytes 5242880 | tf_op jit(solution)/shard_map/all_gather | solution.py:254
  524.2 70.0 %copy-start.61 = (f32[1024]{0:T(1024)S(1)}, f32[1024]{0:T(1024)}, u32[]{:S(2)}) copy-start(f32[1024]{0:T(1024)} %param.39) | copy-start | bytes 12292
  524.2 138.5 %reduce-scatter.12.cloned.1.call-start = ((), (), s32[]{:S(2)}) async-start(), calls=%async_computation.14 | async-start | bytes 5242880 | tf_op jit(solution)/shard_map/reduce_scatter | solution.py:262
  617.9 88.7 %all-gather.22.cloned.1.call-start = ((), (), s32[]{:S(2)}) async-start(), calls=%async_computation.15 | async-start | bytes 5242880 | tf_op jit(solution)/shard_map/all_gather | solution.py:272
  672.0 287.5 %all-gather.24.cloned.1.call-start = ((), (), s32[]{:S(2)}) async-start(), calls=%async_computation.17 | async-start | bytes 2621440 | tf_op jit(solution)/shard_map/all_gather | solution.py:306
  898.7 233.4 %all-reduce.9.cloned.1.call-start = ((), (), s32[]{:S(2)}) async-start(), calls=%async_computation.18 | async-start | bytes 12058624 | tf_op jit(solution)/shard_map/psum | solution.py:314
  923.9 254.2 %reduce-scatter.14.cloned.1.call-start = ((), (), s32[]{:S(2)}) async-start(), calls=%async_computation.16 | async-start | bytes 5242880 | tf_op jit(solution)/shard_map/reduce_scatter | solution.py:297
  (77 other events, 865.3 us)
Sparse Core Ops, SparseCore 0:
  9.6 25.2 all-gather.11
  37.0 34.4 all-gather.9
  220.0 44.5 reduce-scatter.5
  268.7 34.4 all-gather.13
  316.3 44.5 reduce-scatter.7
  367.5 34.4 all-gather.15
  474.9 44.5 reduce-scatter.9
  523.6 34.4 all-gather.17
  559.7 34.4 all-gather.19
  618.0 44.5 reduce-scatter.11
  672.1 34.4 all-gather.21
  898.8 22.5 all-gather.23
  927.2 204.8 all-reduce.8
  1134.5 43.6 reduce-scatter.13
where the time goes:
time: 1250 us; the launch traced here: 1230 us
  waiting for transfers between devices  594 us (48%)
  matrix products  280 us (22%)
  other arithmetic  162 us (13%)
  local copies, waits for them, and re-layouts  99.3 us (8%)
  blocking collectives  62.6 us (5%)
  loops' own time  16.5 us (1%)
  between operations  15.2 us (1%)
    psum x1, waiting for transfers between devices, body(): lax.psum(grad_qkv_weight.astype(jnp.bfloat16), 'dp').astype(jnp.float32)  170 us
    reduce_scatter x2, waiting for transfers between devices, run_forward(): lax.psum_scatter(jnp.dot(picked, out_flat, preferred_element_type=jnp.flo...  88.7 us
    dot_general x12, matrix products, one_block(): jnp.einsum('qhd,khd->hqk', query_blk, key_blk, preferred_element_type=jnp...  78.7 us
    all_gather x2, waiting for transfers between devices, run_forward(): rows_two = lax.all_gather(normed_two, 'mp', axis=0, tiled=True)  68.4 us
    all_gather x2, waiting for transfers between devices, run_forward(): rows_one = lax.all_gather(normed_one, 'mp', axis=0, tiled=True)  67.9 us
    sub x4, other arithmetic, one_block(): weights = jnp.exp(scores - top_score)  64.7 us
    dot_general x8, matrix products, one_block(): jnp.einsum('hqk,khd->qhd', probs, value_blk, preferred_element_type=jnp.f...  47.8 us
    reduce_scatter x1, waiting for transfers between devices, run_forward(): lax.psum_scatter(jnp.dot(picked, down_weight, preferred_element_type=jnp....  44.7 us
  transfers between devices with their start and end apart: 14, of which 13 were waited for; matrix products, arithmetic and copies ran while one was open for 6% of the time, Pallas kernels for 0%

commit v1 on v0

--- a/solution.py
+++ b/solution.py
@@ -178,7 +178,9 @@
     def run_forward(layer_in):
         inputs_f = layer_in.astype(jnp.float32)
         normed_one = layer_norm(inputs_f, attn_norm_gain, attn_norm_bias).astype(jnp.bfloat16)
-        rows_one = lax.all_gather(normed_one, "mp", axis=0, tiled=True)
+        rows_one = jnp.concatenate(
+            lax.all_to_all(jnp.stack([normed_one] * lax.axis_size("mp")), "mp", 0, 0), axis=0
+        )
         projected = jnp.dot(rows_one, qkv_flat, preferred_element_type=jnp.float32)
         projected = projected.reshape(group_rows, pairs_dev, 5, head_size)
         queries = (projected[:, :, 0:2] + qv_bias[None, :, 0:2]).astype(jnp.bfloat16)

time: 1250 us -> 1280 us (1.024)
  waiting for transfers between devices: 594 us -> 611 us
    all_to_all x0 -> x2, waiting for transfers between devices: none -> 107 us  [run_forward(): lax.all_to_all(jnp.stack([normed_one] * lax.axis_size('mp')), 'mp', 0, 0)]
    all_gather x2 -> x0, waiting for transfers between devices: 67.9 us -> none  [run_forward(): rows_one = lax.all_gather(normed_one, 'mp', axis=0, tiled=True)]
    all_gather x1, waiting for transfers between devices: 21.6 us -> 0.02 us  [body(): all_first = lax.all_gather(first_values, 'mp', axis=1, tiled=True)]
  transfers between devices with their start and end apart: 14 -> 14, of which waited for: 13 -> 12; matrix products, arithmetic and copies ran while one was open for 6% -> 6% of each run, Pallas kernels for 0% -> 0%
where the time goes in v1:
time: 1280 us; the launch traced here: 1270 us
  waiting for transfers between devices  611 us (48%)
  matrix products  282 us (22%)
  other arithmetic  163 us (13%)
  local copies, waits for them, and re-layouts  106 us (8%)
  blocking collectives  62.5 us (5%)
  loops' own time  16.5 us (1%)
  between operations  15.4 us (1%)
    psum x1, waiting for transfers between devices, body(): lax.psum(grad_qkv_weight.astype(jnp.bfloat16), 'dp').astype(jnp.float32)  168 us
    all_to_all x2, waiting for transfers between devices, run_forward(): lax.all_to_all(jnp.stack([normed_one] * lax.axis_size('mp')), 'mp', 0, 0)  107 us
    reduce_scatter x2, waiting for transfers between devices, run_forward(): lax.psum_scatter(jnp.dot(picked, out_flat, preferred_element_type=jnp.flo...  89.8 us
    dot_general x12, matrix products, one_block(): jnp.einsum('qhd,khd->hqk', query_blk, key_blk, preferred_element_type=jnp...  78.7 us
    all_gather x2, waiting for transfers between devices, run_forward(): rows_two = lax.all_gather(normed_two, 'mp', axis=0, tiled=True)  68.4 us
    sub x4, other arithmetic, one_block(): weights = jnp.exp(scores - top_score)  64.4 us
    dot_general x8, matrix products, one_block(): jnp.einsum('hqk,khd->qhd', probs, value_blk, preferred_element_type=jnp.f...  47.8 us
    reduce_scatter x1, waiting for transfers between devices, run_forward(): lax.psum_scatter(jnp.dot(picked, down_weight, preferred_element_type=jnp....  44.7 us
  transfers between devices with their start and end apart: 14, of which 12 were waited for; matrix products, arithmetic and copies ran while one was open for 6% of the time, Pallas kernels for 0%

profile of v1, /device:TPU:0, one launch (start us, length us, event | category | flops | bytes accessed | tf_op | source)
XLA Modules:
  0.0 1268.2 jit_solution(9398955872355942945)
XLA Ops:
  20.5 58.9 %all-to-all-done = bf16[4,512,1024]{2,1,0:T(8,128)(2,1)} async-done(((bf16[4,512,1024]{2,1,0:T(8,128)(2,1)}), bf16[4,512,1024]{2,1,0:T(8,128)(2,1)}, u32[]{:S(2)}, u32[]{:S(2)}) %all-to-all-start) | async-done | bytes 4194336 | tf_op jit(solution)/shard_map/all_to_all | solution.py:182
  96.6 132.2 %while.42 = (s32[]{:T(128)}, bf16[4,512,4,64]{1,3,2,0:T(8,128)(2,1)}, s32[4]{0:T(128)S(1)}, bf16[3072,4,64]{0,2,1:T(8,128)(2,1)}, s32[2048]{0:T(1024)S(1)}, /*in...) while((s32[]{:T(128)}, ...), condition=%wide.region_7.9_spmd, body=%wide.region_4.8_spmd.sunk | while | flops 832966144 | bytes 60332316 | solution.py:79
  106.2 16.1 %fusion.194 = (f32[4,512]{1,0:T(4,128)S(1)}, f32[4,512,1536]{2,1,0:T(8,128)}) fusion(f32[4,512,1536]{2,1,0:T(8,128)} %fusion.193, pred[512,1536]{1,0:T(8,128)(4,1)S(1)} %compare_and_fusion.8), kind=kOutput, calls=%fused_computation.221.clone.1 | output fusion | flops 18875904 | bytes 25960448 | tf_op jit(solution)/shard_map/while/body/eval_jaxpr/sub | solution.py:73
  139.2 16.1 %fusion.194 = (f32[4,512]{1,0:T(4,128)S(1)}, f32[4,512,1536]{2,1,0:T(8,128)}) fusion(f32[4,512,1536]{2,1,0:T(8,128)} %fusion.193, pred[512,1536]{1,0:T(8,128)(4,1)S(1)} %compare_and_fusion.8), kind=kOutput, calls=%fused_computation.221.clone.1 | output fusion | flops 18875904 | bytes 25960448 | tf_op jit(solution)/shard_map/while/body/eval_jaxpr/sub | solution.py:73
  172.3 16.1 %fusion.194 = (f32[4,512]{1,0:T(4,128)S(1)}, f32[4,512,1536]{2,1,0:T(8,128)}) fusion(f32[4,512,1536]{2,1,0:T(8,128)} %fusion.193, pred[512,1536]{1,0:T(8,128)(4,1)S(1)} %compare_and_fusion.8), kind=kOutput, calls=%fused_computation.221.clone.1 | output fusion | flops 18875904 | bytes 25960448 | tf_op jit(solution)/shard_map/while/body/eval_jaxpr/sub | solution.py:73
  205.3 16.1 %fusion.194 = (f32[4,512]{1,0:T(4,128)S(1)}, f32[4,512,1536]{2,1,0:T(8,128)}) fusion(f32[4,512,1536]{2,1,0:T(8,128)} %fusion.193, pred[512,1536]{1,0:T(8,128)(4,1)S(1)} %compare_and_fusion.8), kind=kOutput, calls=%fused_computation.221.clone.1 | output fusion | flops 18875904 | bytes 25960448 | tf_op jit(solution)/shard_map/while/body/eval_jaxpr/sub | solution.py:73
  234.8 45.6 %reduce-scatter.6.cloned.1.call-done = bf16[512,1024]{1,0:T(8,128)(2,1)} async-done(((bf16[2048,1024]{1,0:T(8,128)(2,1)}), bf16[512,1024]{1,0:T(8,128)(2,1)}) %reduce-scatter.6.cloned.1.call-update) | async-done | bytes 1048592 | tf_op jit(solution)/shard_map/reduce_scatter | solution.py:198
  284.4 34.6 %all-gather.10.cloned.1.call-done = bf16[2048,1024]{1,0:T(8,128)(2,1)} async-done(((bf16[512,1024]{1,0:T(8,128)(2,1)}), bf16[2048,1024]{1,0:T(8,128)(2,1)}) %all-gather.10.cloned.1.call-update) | async-done | bytes 4194320 | tf_op jit(solution)/shard_map/all_gather | solution.py:207
  318.9 12.9 %fusion.75 = bf16[2048,1024]{1,0:T(8,128)(2,1)} fusion(bf16[1024,1024]{1,0:T(8,128)(2,1)} %param.40, f32[1024]{0:T(1024)S(1)} %copy-done.59, bf16[2048,1024]{1,0:T(8,128)(2,1)} %all-gather.10.cloned.1.call-done, bf16[1024,1024]{1,0:T(8,128)(2,1)S(1)} %copy-done), kind=kOutput, calls=%fused_computation.100 | convolution fusion | flops 8613003264 | bytes 12587008 | tf_op jit(solution)/shard_map/dot_general | solution.py:214
  331.9 44.7 %reduce-scatter.8.cloned.1.call-done = bf16[512,1024]{1,0:T(8,128)(2,1)} async-done(((bf16[2048,1024]{1,0:T(8,128)(2,1)}), bf16[512,1024]{1,0:T(8,128)(2,1)}) %reduce-scatter.8.cloned.1.call-update) | async-done | bytes 1048592 | tf_op jit(solution)/shard_map/reduce_scatter | solution.py:213
  389.9 47.9 %all-to-all-done.1 = bf16[4,512,1024]{2,1,0:T(8,128)(2,1)} async-done(((bf16[4,512,1024]{2,1,0:T(8,128)(2,1)}), bf16[4,512,1024]{2,1,0:T(8,128)(2,1)}, u32[]{:S(2)}, u32[]{:S(2)}) %all-to-all-start.1) | async-done | bytes 4194336 | tf_op jit(solution)/shard_map/all_to_all | solution.py:182
  448.2 55.7 %while.43 = (s32[]{:T(128)}, bf16[4,512,4,64]{1,3,2,0:T(8,128)(2,1)}, f32[4,4,512]{2,1,0:T(4,128)S(1)}, s32[4]{0:T(128)S(1)}, bf16[3072,4,64]{0,2,1:T(8,128)(2,1...) while((s32[]{:T(128)}, ...), condition=%wide.region_17.19_spmd, body=%wide.region_14.18_spmd.sunk | while | flops 845545472 | bytes 49371432 | solution.py:79
  511.1 44.2 %reduce-scatter.10.cloned.1.call-done = bf16[512,1024]{1,0:T(8,128)(2,1)} async-done(((bf16[2048,1024]{1,0:T(8,128)(2,1)}), bf16[512,1024]{1,0:T(8,128)(2,1)}) %reduce-scatter.10.cloned.1.call-update) | async-done | bytes 1048592 | tf_op jit(solution)/shard_map/reduce_scatter | solution.py:198
  560.1 33.8 %all-gather.12.cloned.1.call-done = bf16[2048,1024]{1,0:T(8,128)(2,1)} async-done(((bf16[512,1024]{1,0:T(8,128)(2,1)}), bf16[2048,1024]{1,0:T(8,128)(2,1)}) %all-gather.12.cloned.1.call-update) | async-done | bytes 4194320 | tf_op jit(solution)/shard_map/all_gather | solution.py:207
  602.9 27.1 %all-gather.14.cloned.1.call-done = bf16[2048,1024]{1,0:T(8,128)(2,1)} async-done(((bf16[512,1024]{1,0:T(8,128)(2,1)}), bf16[2048,1024]{1,0:T(8,128)(2,1)}) %all-gather.14.cloned.1.call-update) | async-done | bytes 4194320 | tf_op jit(solution)/shard_map/all_gather | solution.py:256
  630.0 15.5 %fusion.136 = (bf16[1024]{0:T(1024)(128)(2,1)}, bf16[2048,1024]{1,0:T(8,128)(2,1)S(1)}) fusion(f32[2048,1024]{1,0:T(8,128)} %fusion.141, f32[1024]{0:T(1024)S(1)} %copy-done.60, bf16[2048,1024]{1,0:T(8,128)(2,1)} %all-gather.14.cloned.1.call-done, bf16[1024,1024]{1,0:T(8,128)(2,1)} %param.40), kind=kOutput, calls=%fused_computation.219 | convolution fusion | flops 4349492224 | bytes 18880512 | tf_op jit(solution)/shard_map/dot_general | solution.py:45
  654.0 44.5 %reduce-scatter.12.cloned.1.call-done = bf16[512,1024]{1,0:T(8,128)(2,1)} async-done(((bf16[2048,1024]{1,0:T(8,128)(2,1)}), bf16[512,1024]{1,0:T(8,128)(2,1)}) %reduce-scatter.12.cloned.1.call-update) | async-done | bytes 1048592 | tf_op jit(solution)/shard_map/reduce_scatter | solution.py:264
  717.4 25.1 %all-gather.16.cloned.1.call-done = bf16[2048,1024]{1,0:T(8,128)(2,1)} async-done(((bf16[512,1024]{1,0:T(8,128)(2,1)}), bf16[2048,1024]{1,0:T(8,128)(2,1)}) %all-gather.16.cloned.1.call-update) | async-done | bytes 4194320 | tf_op jit(solution)/shard_map/all_gather | solution.py:274
  751.0 180.8 %while.44 = (s32[]{:T(128)}, f32[3072,4,64]{0,2,1:T(8,128)}, f32[3072,4,64]{0,2,1:T(8,128)}, bf16[4,512,4,64]{1,0,3,2:T(4,128)(2,1)}, s32[4]{0:T(128)S(1)}, /*in...) while((s32[]{:T(128)}, f32[3072,4,64]{0,2,1:T(8,128)}, ...), condition=%wide.region_26.28_spmd, body=%wide.region_24.27_spmd.sunk | while | flops 2045378560 | bytes 163641856 | solution.py:133
  934.9 11.9 fusion.105
  973.5 22.6 %all-reduce.5 = (bf16[2,3,64]{2,1,0:T(4,128)(2,1)S(1)}, bf16[1024]{0:T(1024)(128)(2,1)S(1)}) all-reduce(bf16[2,3,64]{2,1,0:T(4,128)(2,1)S(1)} %pad_maximum_fusion.2, bf16[1024]{0:T(1024)(128)(2,1)S(1)} %copy-done.54), channel_id=1, replica_groups=mesh['dp'=8,'mp'=4] {'dp'}, use_global_device_ids=true, to_apply=%region_38.40 | all-reduce | flops 1408 | bytes 5632 | tf_op jit(solution)/shard_map/psum | solution.py:317
  1000.5 167.5 %all-reduce.9.cloned.1.call-done = (bf16[1024,2,5,64]{0,3,2,1:T(8,128)(2,1)}, bf16[2,2,64,1024]{3,2,1,0:T(8,128)(2,1)}, bf16[1024,1024]{1,0:T(8,128)(2,1)}, bf16[1024,1024]{1,0:T(8,128)(2,1)}) async-done(((bf16[1024,2,5,64]{0,3,2,1:T(8,128)(2,1)}, bf16[2,2,64,1024]{3,2,1,0:T(8,128)(2,1)}, bf16[1024,1024]{1,0:T(8,128)(2,1)}, bf16[1024,1024]{1,0:T(8,128)(2,1)}), (bf16[1024,2,5,64]{0,3,2,1:T(8,128)(2,1)}, ...) | async-done | bytes 6029328 | tf_op jit(solution)/shard_map/psum | solution.py:316
  1178.9 35.2 %reduce-scatter.14.cloned.1.call-done = bf16[512,1024]{1,0:T(8,128)(2,1)} async-done(((bf16[2048,1024]{1,0:T(8,128)(2,1)}), bf16[512,1024]{1,0:T(8,128)(2,1)}) %reduce-scatter.14.cloned.1.call-update) | async-done | bytes 1048592 | tf_op jit(solution)/shard_map/reduce_scatter | solution.py:299
  1217.3 39.9 %all-reduce.4 = (f32[1024]{0:T(1024)}, f32[1024]{0:T(1024)}, f32[1024]{0:T(1024)}, f32[1024]{0:T(1024)}, f32[1024]{0:T(1024)}, /*index=5*/f32[1024]{0:T(1024)}) all-reduce(f32[1024]{0:T(1024)S(1)} %get-tuple-element.386, f32[1024]{0:T(1024)S(1)} %get-tuple-element.390, ...), channel_id=1, replica_groups=mesh['dp'=8,'mp'=4] {'dp','mp'}, use_global_device_ids=true, to_apply=%region_32.34 | all-reduce | flops 6144 | bytes 49152 | tf_op jit(solution)/shard_map/psum | solution.py:323
  (421 shorter events, 459.9 us)
Async XLA Ops:
  7.2 311.8 %copy-start = (bf16[1024,1024]{1,0:T(8,128)(2,1)S(1)}, bf16[1024,1024]{1,0:T(8,128)(2,1)}, u32[]{:S(2)}) copy-start(bf16[1024,1024]{1,0:T(8,128)(2,1)} %param.38) | copy-start | bytes 6291460
  14.3 65.1 %all-to-all-start = ((bf16[4,512,1024]{2,1,0:T(8,128)(2,1)}), bf16[4,512,1024]{2,1,0:T(8,128)(2,1)}, u32[]{:S(2)}, u32[]{:S(2)}) async-start(bf16[4,512,1024]{2,1,0:T(8,128)(2,1)} %stack.10), calls=%async_computation | async-start | bytes 8388608 | tf_op jit(solution)/shard_map/all_to_all | solution.py:182
  19.3 67.5 %all-gather.8.cloned.1.call-start = ((), (), s32[]{:S(2)}) async-start(), calls=%async_computation.7 | async-start | bytes 2621440 | tf_op jit(solution)/shard_map/all_gather | solution.py:172
  20.0 260.4 %reduce-scatter.6.cloned.1.call-start = ((), (), s32[]{:S(2)}) async-start(), calls=%async_computation.8 | async-start | bytes 5242880 | tf_op jit(solution)/shard_map/reduce_scatter | solution.py:198
  20.2 66.3 %copy-start.41 = (f32[2,2,64]{2,1,0:T(2,128)}, f32[2,2,64]{2,1,0:T(2,128)S(1)}, u32[]{:S(2)}) copy-start(f32[2,2,64]{2,1,0:T(2,128)S(1)} %copy.44) | copy-start | bytes 3076
  20.5 65.1 %copy-start.50 = (f32[2,64]{1,0:T(2,128)}, f32[2,64]{1,0:T(2,128)S(1)}, u32[]{:S(2)}) copy-start(f32[2,64]{1,0:T(2,128)S(1)} %slice_bitcast_fusion) | copy-start | bytes 1540
  234.5 48.2 %copy-start.31 = (f32[1024]{0:T(1024)S(1)}, f32[1024]{0:T(1024)}, u32[]{:S(2)}) copy-start(f32[1024]{0:T(1024)} %param.36) | copy-start | bytes 12292
  234.5 48.2 %copy-start.44 = (f32[1024]{0:T(1024)S(1)}, f32[1024]{0:T(1024)}, u32[]{:S(2)}) copy-start(f32[1024]{0:T(1024)} %param.37) | copy-start | bytes 12292
  234.5 84.4 %all-gather.10.cloned.1.call-start = ((), (), s32[]{:S(2)}) async-start(), calls=%async_computation.9 | async-start | bytes 5242880 | tf_op jit(solution)/shard_map/all_gather | solution.py:207
  284.3 92.3 %reduce-scatter.8.cloned.1.call-start = ((), (), s32[]{:S(2)}) async-start(), calls=%async_computation.10 | async-start | bytes 5242880 | tf_op jit(solution)/shard_map/reduce_scatter | solution.py:213
  331.9 49.8 %copy-start.33 = (f32[1024]{0:T(1024)S(1)}, f32[1024]{0:T(1024)}, u32[]{:S(2)}) copy-start(f32[1024]{0:T(1024)} %param.30) | copy-start | bytes 12292
  331.9 49.7 %copy-start.43 = (f32[1024]{0:T(1024)S(1)}, f32[1024]{0:T(1024)}, u32[]{:S(2)}) copy-start(f32[1024]{0:T(1024)} %param.31) | copy-start | bytes 12292
  384.7 53.0 %all-to-all-start.1 = ((bf16[4,512,1024]{2,1,0:T(8,128)(2,1)}), bf16[4,512,1024]{2,1,0:T(8,128)(2,1)}, u32[]{:S(2)}, u32[]{:S(2)}) async-start(bf16[4,512,1024]{2,1,0:T(8,128)(2,1)} %stack.13), calls=%async_computation.3 | async-start | bytes 8388608 | tf_op jit(solution)/shard_map/all_to_all | solution.py:182
  389.6 165.8 %reduce-scatter.10.cloned.1.call-start = ((), (), s32[]{:S(2)}) async-start(), calls=%async_computation.11 | async-start | bytes 5242880 | tf_op jit(solution)/shard_map/reduce_scatter | solution.py:198
  510.7 47.1 %copy-start.32 = (f32[1024]{0:T(1024)S(1)}, f32[1024]{0:T(1024)}, u32[]{:S(2)}) copy-start(f32[1024]{0:T(1024)} %param.36) | copy-start | bytes 12292
  510.7 47.1 %copy-start.45 = (f32[1024]{0:T(1024)S(1)}, f32[1024]{0:T(1024)}, u32[]{:S(2)}) copy-start(f32[1024]{0:T(1024)} %param.37) | copy-start | bytes 12292
  510.7 83.3 %all-gather.12.cloned.1.call-start = ((), (), s32[]{:S(2)}) async-start(), calls=%async_computation.12 | async-start | bytes 5242880 | tf_op jit(solution)/shard_map/all_gather | solution.py:207
  559.3 70.7 %all-gather.14.cloned.1.call-start = ((), (), s32[]{:S(2)}) async-start(), calls=%async_computation.13 | async-start | bytes 5242880 | tf_op jit(solution)/shard_map/all_gather | solution.py:256
  560.1 69.9 %copy-start.60 = (f32[1024]{0:T(1024)S(1)}, f32[1024]{0:T(1024)}, u32[]{:S(2)}) copy-start(f32[1024]{0:T(1024)} %param.39) | copy-start | bytes 12292
  560.1 138.4 %reduce-scatter.12.cloned.1.call-start = ((), (), s32[]{:S(2)}) async-start(), calls=%async_computation.14 | async-start | bytes 5242880 | tf_op jit(solution)/shard_map/reduce_scatter | solution.py:264
  653.8 88.7 %all-gather.16.cloned.1.call-start = ((), (), s32[]{:S(2)}) async-start(), calls=%async_computation.15 | async-start | bytes 5242880 | tf_op jit(solution)/shard_map/all_gather | solution.py:274
  707.8 289.4 %all-gather.18.cloned.1.call-start = ((), (), s32[]{:S(2)}) async-start(), calls=%async_computation.17 | async-start | bytes 2621440 | tf_op jit(solution)/shard_map/all_gather | solution.py:308
  934.6 233.4 %all-reduce.9.cloned.1.call-start = ((), (), s32[]{:S(2)}) async-start(), calls=%async_computation.18 | async-start | bytes 12058624 | tf_op jit(solution)/shard_map/psum | solution.py:316
  961.8 252.2 %reduce-scatter.14.cloned.1.call-start = ((), (), s32[]{:S(2)}) async-start(), calls=%async_computation.16 | async-start | bytes 5242880 | tf_op jit(solution)/shard_map/reduce_scatter | solution.py:299
  (76 other events, 841.7 us)
Sparse Core Ops, SparseCore 0:
  21.6 37.0 all-gather.7
  234.6 45.6 reduce-scatter.5
  284.4 34.4 all-gather.9
  332.0 44.5 reduce-scatter.7
  510.8 44.5 reduce-scatter.9
  559.5 34.4 all-gather.11
  595.5 34.4 all-gather.13
  653.9 44.5 reduce-scatter.11
  708.0 34.4 all-gather.15
  934.7 22.5 all-gather.17
  963.1 204.8 all-reduce.8
  1170.4 43.6 reduce-scatter.13
